TPU v7x, 32 devices: a whole 2x2x4 slice. The times are simulated.
32 devices in a mesh: bits: 16 (over z, y, x), docs: 2 (over core).
Axes of the slice: x: 2, y: 2, z: 4, core: 2. Of those that a mesh axis runs over, the one named last changes fastest.
Arguments:
- positions: int32 [1024, 4096], P(('bits', 'docs')), may hold values from 0 to 4095
- element_weights: float32 [1024, 1024], P(('bits', 'docs')), may hold values from 0.25 to 4
- set_sizes: int32 [1024], P(('bits', 'docs')), may hold values from 256 to 1024, as said below
- bit_weights: bfloat16 [4096], replicated, may hold values from 0.25 to 4
- candidates: int32 [2, 16, 16], P('docs'), may hold values from 0 to 63, as said below
Outputs:
- scores: float32 [2, 16, 128, 64], P('docs', 'bits')
Inputs may be any that keep to these rules, and one draw needn't show every extreme that they name: `set_sizes`: one document in every draw has exactly 1024 elements. `candidates`: the 16 row tiles named for one block are distinct. `positions`: entries of a row beyond its first 4 * set_sizes are not part of the filter.
All inputs are finite; a program needn't handle non-finite values.
Results may differ from a plain program's by a relative error of at most 0.0012.
Values may be sent and summed in bfloat16 or wider, within the bound.
A program may use at most 64 MiB of HBM per device.

v0:
```python
import math

import jax
import jax.numpy as jnp
from jax import lax
from jax.sharding import PartitionSpec as P

FILTER_BITS = 4096
HASHES = 4
TILE = 8


def build_filter(positions, element_weights, set_sizes):
    doc_count, slot_count = positions.shape
    elem_count = element_weights.shape[1]
    low_cells = 64
    high_cells = FILTER_BITS // low_cells
    slot_index = jnp.arange(slot_count, dtype=jnp.int32)
    usable = slot_index[None, :] < HASHES * set_sizes[:, None]
    spread = jnp.broadcast_to(element_weights[:, :, None], (doc_count, elem_count, HASHES)).reshape(
        doc_count, slot_count
    )
    slot_weights = jnp.where(usable, spread, 0.0)
    upper = slot_weights.astype(jnp.bfloat16)
    remain = slot_weights - upper.astype(jnp.float32)
    middle = remain.astype(jnp.bfloat16)
    lower = (remain - middle.astype(jnp.float32)).astype(jnp.bfloat16)
    weight_parts = jnp.stack([upper, middle, lower], axis=1)
    high_index = positions // low_cells
    low_index = positions - high_index * low_cells
    group = math.gcd(doc_count, 8)

    def one_group(inputs):
        part_block, high_block, low_block = inputs
        high_onehot = (high_block[:, :, None] == jnp.arange(high_cells, dtype=jnp.int32)).astype(
            jnp.bfloat16
        )
        low_onehot = (low_block[:, :, None] == jnp.arange(low_cells, dtype=jnp.int32)).astype(
            jnp.bfloat16
        )
        left = part_block[:, :, :, None] * high_onehot[:, None, :, :]
        summed = jnp.einsum("dcph,dpl->dhl", left, low_onehot, preferred_element_type=jnp.float32)
        return summed.reshape(group, FILTER_BITS)

    grouped = lax.map(
        one_group,
        (
            weight_parts.reshape(doc_count // group, group, 3, slot_count),
            high_index.reshape(doc_count // group, group, slot_count),
            low_index.reshape(doc_count // group, group, slot_count),
        ),
    )
    return grouped.reshape(doc_count, FILTER_BITS).astype(jnp.bfloat16)


def weighted_pop(cells, weights):
    weighted = cells * weights
    return jnp.sum(weighted.astype(jnp.float32) * cells.astype(jnp.float32), axis=1)


def estimate(shared, pop_rows, pop_cols, size_rows, size_cols):
    union_weight = pop_rows[:, None] + pop_cols[None, :] - shared
    ratio = shared / union_weight
    smaller = jnp.minimum(size_rows[:, None], size_cols[None, :])
    return ratio * (size_rows[:, None] + size_cols[None, :]) / ((1.0 + ratio) * smaller)


def pick_tiles(slice_cells, tile_choice, row_group, groups, row_half):
    width = slice_cells.shape[1]
    row_tiles = row_half // TILE
    tiles = slice_cells.reshape(groups, row_tiles, TILE * width)
    own_tiles = lax.dynamic_index_in_dim(tiles, row_group, 0, keepdims=False)
    onehot = (tile_choice[:, :, None] == jnp.arange(row_tiles, dtype=jnp.int32)).astype(
        jnp.bfloat16
    )
    picked = jnp.einsum("jcr,rw->jcw", onehot, own_tiles, preferred_element_type=jnp.float32)
    return picked.astype(jnp.bfloat16).reshape(
        tile_choice.shape[0], tile_choice.shape[1] * TILE, width
    )


def body(positions, element_weights, set_sizes, bit_weights, candidates):
    col_index = lax.axis_index("bits")
    row_group = lax.axis_index("docs")
    blocks = lax.axis_size("bits")
    groups = lax.axis_size("docs")
    doc_total = positions.shape[0] * blocks * groups
    row_half = doc_total // groups
    col_width = doc_total // blocks
    slot_count = candidates.shape[2] * TILE
    tile_offsets = jnp.arange(TILE, dtype=jnp.int32)
    own_cells = build_filter(positions, element_weights, set_sizes)
    local_pop = weighted_pop(own_cells, bit_weights)
    every_pop, size_float = (
        lax.all_gather(local_pop, ("bits", "docs"), axis=0, tiled=True),
        lax.all_gather(set_sizes.astype(jnp.float32), ("bits", "docs"), axis=0, tiled=True),
    )
    pair_cells = lax.all_gather(own_cells, "docs", axis=0, tiled=True)
    slice_cells = lax.all_to_all(pair_cells, "bits", split_axis=1, concat_axis=0, tiled=True)
    tile_rows = row_group * row_half + (candidates[0][:, :, None] * TILE + tile_offsets).reshape(
        blocks, slot_count
    )
    picked_cells = pick_tiles(slice_cells, candidates[0], row_group, groups, row_half)
    row_cells = lax.all_to_all(picked_cells, "bits", split_axis=0, concat_axis=2, tiled=True)[0]
    shared = lax.dot_general(
        row_cells * bit_weights,
        pair_cells,
        (((1,), (1,)), ((), ())),
        preferred_element_type=jnp.float32,
    )
    row_docs = lax.dynamic_index_in_dim(tile_rows, col_index, 0, keepdims=False)
    pop_rows = every_pop[row_docs]
    pop_cols = lax.dynamic_slice_in_dim(every_pop, col_index * col_width, col_width, 0)
    size_rows = size_float[row_docs]
    size_cols = lax.dynamic_slice_in_dim(size_float, col_index * col_width, col_width, 0)
    scores = estimate(shared, pop_rows, pop_cols, size_rows, size_cols)
    return scores.reshape(1, 1, slot_count, col_width)


def solution(mesh):
    return jax.shard_map(
        body,
        mesh=mesh,
        in_specs=(
            P(("bits", "docs"), None),
            P(("bits", "docs"), None),
            P(("bits", "docs")),
            P(),
            P("docs", None, None),
        ),
        out_specs=P("docs", "bits", None, None),
        check_vma=False,
    )
```

profile of v0, /device:TPU:0, one launch (start us, length us, event | category | flops | bytes accessed | tf_op | source)
XLA Modules:
  0.0 158.0 jit_solution(18137033540736739117)
XLA Ops:
  0.0 1.1 copy.33
  1.1 0.4 broadcast_in_dim.12
  1.5 5.7 %reshape.175 = f32[4,8,1,4096]{1,0,3,2:T(4,128)} reshape(f32[32,1024,4]{0,2,1:T(4,128)S(1)} %broadcast_in_dim.12) | data formatting | bytes 1048576 | tf_op jit(solution)/shard_map/reshape | solution.py:20
  7.2 0.0 copy-start.3
  7.2 0.0 copy-start
  7.2 6.7 %copy.34 = f32[4,8,1,4096]{3,1,2,0:T(8,128)S(1)} copy(f32[4,8,1,4096]{1,0,3,2:T(4,128)} %reshape.175) | data formatting | bytes 1048576 | tf_op jit(solution)/shard_map/reshape | solution.py:20
  13.9 0.0 copy-done.3
  13.9 0.1 lt.60
  14.0 0.2 fusion.7
  14.1 0.1 fusion.6
  14.3 0.0 copy-done
  14.3 0.3 subtract_bitcast_fusion
  14.6 0.1 pad_maximum_fusion
  14.7 0.0 copy-start.2
  14.7 60.3 %while.10 = (s32[]{:T(128)}, bf16[4,8,4096]{2,1,0:T(8,128)(2,1)S(1)}, bf16[4,8,3,4096]{3,1,2,0:T(8,128)(2,1)S(1)}, s32[4,8,4096]{2,1,0:T(8,128)S(1)}, s32[4,8,4096]{2,1,0:T(8,128)S(1)}, /*index=5*/s32[]{:T(128)}) while((s32[]{:T(128)}, bf16[4,8,4096]{2,1,0:T(8,128)(2,1)S(1)}, bf16[4,8,3,4096]{3,1,2,0:T(8,128)(2,1)S(1)}, ...), condition=%wide.region_2.3_spmd, body=%wide.region_0.2_spmd.sunk | while | flops 304087040 | bytes 18874448 | solution.py:45
  14.8 3.0 %fusion.23 = bf16[8,4096,64]{1,2,0:T(8,128)(2,1)} fusion(s32[8,4096]{1,0:T(8,128)S(1)} %get-tuple-element.109), kind=kLoop, calls=%fused_computation.5.clone.1 | loop fusion | flops 4194304 | bytes 4325376 | tf_op jit(solution)/shard_map/while/body/eval_jaxpr/convert_element_type | solution.py:35
  17.8 0.2 copy.46
  18.0 7.9 %convert_reduce_fusion.2 = bf16[8,4096,64]{1,2,0:T(8,128)(2,1)} fusion(bf16[8,4096,64]{1,2,0:T(8,128)(2,1)} %fusion.23, bf16[8,3,4096]{2,1,0:T(4,128)(2,1)S(1)} %bitcast.50), kind=kLoop, calls=%fused_computation.2.clone.1 | loop fusion | flops 29360128 | bytes 8585216 | tf_op jit(solution)/shard_map/while/body/eval_jaxpr/dcph,dpl->dhl/reduce_sum | solution.py:42
  25.9 3.7 %fusion.24 = bf16[8,64,64]{2,1,0:T(8,128)(2,1)S(1)} fusion(bf16[8,4096,64]{1,2,0:T(8,128)(2,1)} %convert_reduce_fusion.2, s32[8,4096]{1,0:T(8,128)S(1)} %get-tuple-element.110), kind=kOutput, calls=%fused_computation.6.clone.1 | convolution fusion | flops 270532608 | bytes 4390912 | tf_op jit(solution)/shard_map/while/body/eval_jaxpr/dcph,dpl->dhl/dot_general | solution.py:42
  29.6 0.2 broadcast_in_dim.31
  29.8 3.0 %fusion.23 = bf16[8,4096,64]{1,2,0:T(8,128)(2,1)} fusion(s32[8,4096]{1,0:T(8,128)S(1)} %get-tuple-element.109), kind=kLoop, calls=%fused_computation.5.clone.1 | loop fusion | flops 4194304 | bytes 4325376 | tf_op jit(solution)/shard_map/while/body/eval_jaxpr/convert_element_type | solution.py:35
  32.9 0.2 copy.46
  33.1 7.9 %convert_reduce_fusion.2 = bf16[8,4096,64]{1,2,0:T(8,128)(2,1)} fusion(bf16[8,4096,64]{1,2,0:T(8,128)(2,1)} %fusion.23, bf16[8,3,4096]{2,1,0:T(4,128)(2,1)S(1)} %bitcast.50), kind=kLoop, calls=%fused_computation.2.clone.1 | loop fusion | flops 29360128 | bytes 8585216 | tf_op jit(solution)/shard_map/while/body/eval_jaxpr/dcph,dpl->dhl/reduce_sum | solution.py:42
  40.9 3.7 %fusion.24 = bf16[8,64,64]{2,1,0:T(8,128)(2,1)S(1)} fusion(bf16[8,4096,64]{1,2,0:T(8,128)(2,1)} %convert_reduce_fusion.2, s32[8,4096]{1,0:T(8,128)S(1)} %get-tuple-element.110), kind=kOutput, calls=%fused_computation.6.clone.1 | convolution fusion | flops 270532608 | bytes 4390912 | tf_op jit(solution)/shard_map/while/body/eval_jaxpr/dcph,dpl->dhl/dot_general | solution.py:42
  44.6 0.2 broadcast_in_dim.31
  44.9 3.0 %fusion.23 = bf16[8,4096,64]{1,2,0:T(8,128)(2,1)} fusion(s32[8,4096]{1,0:T(8,128)S(1)} %get-tuple-element.109), kind=kLoop, calls=%fused_computation.5.clone.1 | loop fusion | flops 4194304 | bytes 4325376 | tf_op jit(solution)/shard_map/while/body/eval_jaxpr/convert_element_type | solution.py:35
  48.0 0.2 copy.46
  48.1 7.9 %convert_reduce_fusion.2 = bf16[8,4096,64]{1,2,0:T(8,128)(2,1)} fusion(bf16[8,4096,64]{1,2,0:T(8,128)(2,1)} %fusion.23, bf16[8,3,4096]{2,1,0:T(4,128)(2,1)S(1)} %bitcast.50), kind=kLoop, calls=%fused_computation.2.clone.1 | loop fusion | flops 29360128 | bytes 8585216 | tf_op jit(solution)/shard_map/while/body/eval_jaxpr/dcph,dpl->dhl/reduce_sum | solution.py:42
  56.0 3.7 %fusion.24 = bf16[8,64,64]{2,1,0:T(8,128)(2,1)S(1)} fusion(bf16[8,4096,64]{1,2,0:T(8,128)(2,1)} %convert_reduce_fusion.2, s32[8,4096]{1,0:T(8,128)S(1)} %get-tuple-element.110), kind=kOutput, calls=%fused_computation.6.clone.1 | convolution fusion | flops 270532608 | bytes 4390912 | tf_op jit(solution)/shard_map/while/body/eval_jaxpr/dcph,dpl->dhl/dot_general | solution.py:42
  59.7 0.2 broadcast_in_dim.31
  60.0 3.0 %fusion.23 = bf16[8,4096,64]{1,2,0:T(8,128)(2,1)} fusion(s32[8,4096]{1,0:T(8,128)S(1)} %get-tuple-element.109), kind=kLoop, calls=%fused_computation.5.clone.1 | loop fusion | flops 4194304 | bytes 4325376 | tf_op jit(solution)/shard_map/while/body/eval_jaxpr/convert_element_type | solution.py:35
  63.0 0.2 copy.46
  63.2 7.9 %convert_reduce_fusion.2 = bf16[8,4096,64]{1,2,0:T(8,128)(2,1)} fusion(bf16[8,4096,64]{1,2,0:T(8,128)(2,1)} %fusion.23, bf16[8,3,4096]{2,1,0:T(4,128)(2,1)S(1)} %bitcast.50), kind=kLoop, calls=%fused_computation.2.clone.1 | loop fusion | flops 29360128 | bytes 8585216 | tf_op jit(solution)/shard_map/while/body/eval_jaxpr/dcph,dpl->dhl/reduce_sum | solution.py:42
  71.1 3.7 %fusion.24 = bf16[8,64,64]{2,1,0:T(8,128)(2,1)S(1)} fusion(bf16[8,4096,64]{1,2,0:T(8,128)(2,1)} %convert_reduce_fusion.2, s32[8,4096]{1,0:T(8,128)S(1)} %get-tuple-element.110), kind=kOutput, calls=%fused_computation.6.clone.1 | convolution fusion | flops 270532608 | bytes 4390912 | tf_op jit(solution)/shard_map/while/body/eval_jaxpr/dcph,dpl->dhl/dot_general | solution.py:42
  74.8 0.2 broadcast_in_dim.31
  75.0 2.3 %all_gather.9 = bf16[64,4096]{1,0:T(8,128)(2,1)S(1)} all-gather(bf16[32,4096]{1,0:T(8,128)(2,1)S(1)} %bitcast.53), channel_id=1, replica_groups=mesh['bits'=16,'docs'=2] {'docs'}, dimensions={0}, use_global_device_ids=true | all-gather | bytes 786432 | tf_op jit(solution)/shard_map/all_gather | solution.py:98
  77.3 0.8 copy.44
  78.1 8.3 %all-to-all-start = ((bf16[64,16,256]{2,0,1:T(8,128)(2,1)}), bf16[64,16,256]{2,0,1:T(8,128)(2,1)S(1)}, u32[]{:S(2)}, u32[]{:S(2)}) async-start(bf16[64,16,256]{2,0,1:T(8,128)(2,1)} %bitcast.43), calls=%async_computation | async-start | bytes 1048576 | tf_op jit(solution)/shard_map/all_to_all | solution.py:99
  86.4 15.4 %all-to-all-done = bf16[64,16,256]{2,0,1:T(8,128)(2,1)S(1)} async-done(((bf16[64,16,256]{2,0,1:T(8,128)(2,1)}), bf16[64,16,256]{2,0,1:T(8,128)(2,1)S(1)}, u32[]{:S(2)}, u32[]{:S(2)}) %all-to-all-start) | async-done | bytes 524320 | tf_op jit(solution)/shard_map/all_to_all | solution.py:99
  101.8 0.0 copy-start.1
  101.8 0.2 reshape.178
  102.0 0.0 copy-done.2
  102.0 0.5 convolution_convert_fusion
  102.5 0.5 reshape.179
  103.1 1.3 copy.37
  104.4 3.9 %all-to-all-start.1 = ((bf16[16,128,256]{1,2,0:T(8,128)(2,1)}), bf16[16,128,256]{1,2,0:T(8,128)(2,1)S(1)}, u32[]{:S(2)}, u32[]{:S(2)}) async-start(bf16[16,128,256]{1,2,0:T(8,128)(2,1)} %copy.37), calls=%async_computation.1 | async-start | bytes 2097152 | tf_op jit(solution)/shard_map/all_to_all | solution.py:104
  108.3 0.0 copy-done.1
  108.3 0.2 multiply_reduce_fusion
  108.5 0.1 reshape.197
  108.6 0.2 dynamic-update-slice
  108.8 0.1 convert_dynamic-update-slice_fusion
  108.9 44.8 %all-reduce.2 = (f32[1024]{0:T(1024)S(1)}, f32[1024]{0:T(1024)S(1)}) all-reduce(f32[1024]{0:T(1024)S(1)} %convert_dynamic-update-slice_fusion, f32[1024]{0:T(1024)S(1)} %dynamic-update-slice), channel_id=1, replica_groups=mesh['bits'=16,'docs'=2] {'bits','docs'}, use_global_device_ids=true, to_apply=%add.1 | all-reduce | flops 2048 | bytes 16384
  153.7 0.1 dynamic_slice.27
  153.7 0.1 dynamic_slice.28
  153.8 0.1 copy.38
  153.9 0.1 add.90
  154.0 0.2 fusion.12
  154.2 1.0 gather_fusion
  155.2 1.0 gather_fusion.1
  156.2 0.0 all-to-all-done.1
  156.2 0.8 bitcast_multiply_fusion
  157.0 1.0 divide_bitcast_fusion
  (21 shorter events, 0.2 us)
Async XLA Ops:
  7.2 6.7 %copy-start.3 = (s32[32]{0:T(128)S(1)}, s32[32]{0:T(128)}, u32[]{:S(2)}) copy-start(s32[32]{0:T(128)} %param.9) | copy-start | bytes 388
  7.2 7.1 %copy-start = (s32[32,4096]{1,0:T(8,128)S(1)}, s32[32,4096]{1,0:T(8,128)}, u32[]{:S(2)}) copy-start(s32[32,4096]{1,0:T(8,128)} %param.7) | copy-start | bytes 1572868
  14.7 87.3 %copy-start.2 = (s32[1,16,16]{2,1,0:T(8,128)S(1)}, s32[1,16,16]{2,1,0:T(8,128)}, u32[]{:S(2)}) copy-start(s32[1,16,16]{2,1,0:T(8,128)} %param.11) | copy-start | bytes 3076
  78.1 23.6 %all-to-all-start = ((bf16[64,16,256]{2,0,1:T(8,128)(2,1)}), bf16[64,16,256]{2,0,1:T(8,128)(2,1)S(1)}, u32[]{:S(2)}, u32[]{:S(2)}) async-start(bf16[64,16,256]{2,0,1:T(8,128)(2,1)} %bitcast.43), calls=%async_computation | async-start | bytes 1048576 | tf_op jit(solution)/shard_map/all_to_all | solution.py:99
  101.8 6.5 %copy-start.1 = (bf16[4096]{0:T(1024)(128)(2,1)S(1)}, bf16[4096]{0:T(1024)(128)(2,1)}, u32[]{:S(2)}) copy-start(bf16[4096]{0:T(1024)(128)(2,1)} %param.10) | copy-start | bytes 24580
  104.4 51.8 %all-to-all-start.1 = ((bf16[16,128,256]{1,2,0:T(8,128)(2,1)}), bf16[16,128,256]{1,2,0:T(8,128)(2,1)S(1)}, u32[]{:S(2)}, u32[]{:S(2)}) async-start(bf16[16,128,256]{1,2,0:T(8,128)(2,1)} %copy.37), calls=%async_computation.1 | async-start | bytes 2097152 | tf_op jit(solution)/shard_map/all_to_all | solution.py:104
where the time goes:
time: 159 us; the launch traced here: 158 us
  blocking collectives  47.1 us (30%)
  other arithmetic  45.5 us (29%)
  local copies, waits for them, and re-layouts  21 us (13%)
  matrix products  16.3 us (10%)
  waiting for transfers between devices  15.4 us (10%)
  starting transfers between devices  12.2 us (8%)
    unnamed x1, blocking collectives  44.8 us
    reduce_sum x4, other arithmetic, one_group(): jnp.einsum('dcph,dpl->dhl', left, low_onehot, preferred_element_type=jnp....  31.4 us
    all_to_all x1, waiting for transfers between devices, body(): lax.all_to_all(pair_cells, 'bits', split_axis=1, concat_axis=0, tiled=True)  15.4 us
    dot_general x4, matrix products, one_group(): jnp.einsum('dcph,dpl->dhl', left, low_onehot, preferred_element_type=jnp....  14.9 us
    reshape x2, local copies, waits for them, and re-layouts, build_filter(): jnp.broadcast_to(element_weights[:, :, None], (doc_count, elem_count, HAS...  12.4 us
    convert_element_type x4, other arithmetic, one_group(): (high_block[:, :, None] == jnp.arange(high_cells, dtype=jnp.int32)).astyp...  12.2 us
    all_to_all x1, starting transfers between devices, body(): lax.all_to_all(pair_cells, 'bits', split_axis=1, concat_axis=0, tiled=True)  8.26 us
    all_to_all x1, starting transfers between devices, body(): lax.all_to_all(picked_cells, 'bits', split_axis=0, concat_axis=2, tiled=T...  3.94 us
  transfers between devices with their start and end apart: 2, of which 1 were waited for; matrix products, arithmetic and copies ran while one was open for 2% of the time, Pallas kernels for 0%

commit v1 on v0

--- a/solution.py
+++ b/solution.py
@@ -1,13 +1,21 @@
+import functools
 import math
 
 import jax
 import jax.numpy as jnp
 from jax import lax
+from jax.experimental import pallas as pl
+from jax.experimental.pallas import tpu as pltpu
 from jax.sharding import PartitionSpec as P
 
 FILTER_BITS = 4096
 HASHES = 4
 TILE = 8
+LANES = 128
+CHUNK = 512
+UNROLL = 4
+PARTS = 2
+MESH = pl.DeviceIdType.MESH
 
 
 def build_filter(positions, element_weights, set_sizes):
@@ -117,9 +125,237 @@
     return scores.reshape(1, 1, slot_count, col_width)
 
 
+NT = (((1,), (1,)), ((), ()))
+
+
+def filter_kernel(sizes_ref, pos_ref, elem_ref, bw_ref, cells_ref, stats_ref, spread, acc, rows):
+    docs, slots = pos_ref.shape
+    elems = elem_ref.shape[1]
+    highs = FILTER_BITS // LANES
+    lane = lax.broadcasted_iota(jnp.int32, (docs, LANES), 1)
+    sub = lax.broadcasted_iota(jnp.int32, (docs, LANES), 0)
+    size_of = jnp.zeros((docs, LANES), jnp.int32)
+    total = jnp.int32(0)
+    for d in range(docs):
+        size = sizes_ref[d]
+        size_of = jnp.where(sub == d, size, size_of)
+        total = total + (HASHES * size + CHUNK - 1) // CHUNK
+    width = 2 * LANES
+    wide = (lax.broadcasted_iota(jnp.int32, (width, HASHES * width), 1) // HASHES
+            == lax.broadcasted_iota(jnp.int32, (width, HASHES * width), 0))
+    wide = jnp.where(wide, 1.0, 0.0).astype(jnp.bfloat16)
+    size_wide = jnp.concatenate([size_of] * (width // LANES), axis=1)
+    lane_wide = lax.broadcasted_iota(jnp.int32, (docs, width), 1)
+    for q in range(elems // width):
+        value = elem_ref[:, q * width:(q + 1) * width]
+        value = jnp.where(lane_wide + q * width < size_wide, value, 0.0)
+        upper = value.astype(jnp.bfloat16)
+        lower = (value - upper.astype(jnp.float32)).astype(jnp.bfloat16)
+        for p, part in enumerate((upper, lower)):
+            spread[p, :, q * HASHES * width:(q + 1) * HASHES * width] = jnp.dot(
+                part, wide, preferred_element_type=jnp.float32)
+
+    @pl.loop(0, docs + 1)
+    def _(d):
+        acc[d] = jnp.zeros(acc.shape[1:], jnp.float32)
+
+    low_iota = lax.broadcasted_iota(jnp.int32, (LANES, CHUNK), 0)
+    high_iota = lax.broadcasted_iota(jnp.int32, (highs, CHUNK), 0)
+
+    def group(_, carry):
+        d, c = carry
+        for _ in range(UNROLL):
+            row = jnp.minimum(d, docs - 1)
+            at = pl.ds(pl.multiple_of(c * CHUNK, CHUNK), CHUNK)
+            pos = pos_ref[pl.ds(row, 1), at]
+            high, low = lax.shift_right_logical(pos, 7), lax.bitwise_and(pos, LANES - 1)
+            left = jnp.where(low == low_iota, 1.0, 0.0).astype(jnp.bfloat16)
+            hit = high == high_iota
+            right = jnp.concatenate(
+                [jnp.where(hit, spread[p, pl.ds(row, 1), at], 0.0) for p in range(PARTS)],
+                axis=0).astype(jnp.bfloat16)
+            acc[d] = acc[d] + lax.dot_general(left, right, NT, preferred_element_type=jnp.float32)
+            more = (c + 1) * CHUNK < HASHES * sizes_ref[row]
+            c = jnp.where(more, c + 1, 0)
+            d = jnp.where(more, d, jnp.minimum(d + 1, docs))
+            c = jnp.where(d == docs, 0, c)
+        return d, c
+
+    lax.fori_loop(0, (total + UNROLL - 1) // UNROLL, group, (jnp.int32(0), jnp.int32(0)))
+
+    @pl.loop(0, docs)
+    def _(d):
+        both = acc[d].T
+        rows[pl.ds(d, highs, stride=docs), :] = both[:highs] + both[highs:]
+
+    span = cells_ref.shape[2]
+    pop = jnp.zeros((docs, LANES), jnp.float32)
+    for h in range(highs):
+        cells = rows[h * docs:(h + 1) * docs, :].astype(jnp.bfloat16)
+        cells_ref[h * LANES // span, :, h * LANES % span:h * LANES % span + LANES] = cells
+        full = cells.astype(jnp.float32)
+        weight = bw_ref[:, h * LANES:(h + 1) * LANES].astype(jnp.float32)
+        pop = pop + (full * weight).astype(jnp.bfloat16).astype(jnp.float32) * full
+    pop = jnp.sum(pop, axis=1, keepdims=True)
+    both = jnp.where(lane == sub, pop, 0.0)
+    both = jnp.where(lane == sub + docs, size_of.astype(jnp.float32), both)
+    stats_ref[...] = jnp.sum(both, axis=0, keepdims=True)
+
+
+def make_filter(positions, element_weights, set_sizes, weights, pieces):
+    docs, slots = positions.shape
+    vmem = pl.BlockSpec(memory_space=pltpu.VMEM)
+    highs = FILTER_BITS // LANES
+    return pl.pallas_call(
+        filter_kernel,
+        out_shape=(
+            jax.ShapeDtypeStruct((pieces, docs, FILTER_BITS // pieces), jnp.bfloat16),
+            jax.ShapeDtypeStruct((1, LANES), jnp.float32),
+        ),
+        in_specs=[pl.BlockSpec(memory_space=pltpu.SMEM), vmem, vmem, vmem],
+        out_specs=(vmem, vmem),
+        scratch_shapes=[
+            pltpu.VMEM((PARTS, docs, slots), jnp.float32),
+            pltpu.VMEM((docs + 1, LANES, PARTS * highs), jnp.float32),
+            pltpu.VMEM((highs * docs, LANES), jnp.float32),
+        ],
+    )(set_sizes, positions, element_weights, weights)
+
+
+def score_kernel(blocks, groups, cand_ref, cells_ref, stats_ref, bw_ref, out_ref,
+                 slab, stat, weighted, part, inbox,
+                 send1, recv1, send1s, recv1s, send2, recv2, send2s, recv2s, send3, recv3):
+    col, grp = lax.axis_index("bits"), lax.axis_index("docs")
+    docs, span = cells_ref.shape[1:]
+    picks = cand_ref.shape[2]
+    owners = blocks * groups
+    row_half = docs * owners // groups
+    width = docs * groups
+    me = col * groups + grp
+
+    barrier = pltpu.get_barrier_semaphore()
+    for k in range(1, blocks):
+        pl.semaphore_signal(barrier, inc=1, device_id=(lax.rem(col + k, blocks), grp), device_id_type=MESH)
+    for k in range(1, groups):
+        pl.semaphore_signal(barrier, inc=1, device_id=(col, lax.rem(grp + k, groups)), device_id_type=MESH)
+    pl.semaphore_wait(barrier, blocks + groups - 2)
+
+    def remote(src, dst, send, recv, device):
+        return pltpu.make_async_remote_copy(
+            src_ref=src, dst_ref=dst, send_sem=send, recv_sem=recv, device_id=device, device_id_type=MESH)
+
+    first = []
+    for k in range(1, blocks):
+        to = lax.rem(col + k, blocks)
+        first.append(remote(cells_ref.at[to], slab.at[me], send1.at[k], recv1.at[k], (to, grp)))
+        first.append(remote(stats_ref.at[0], stat.at[me], send1s.at[k], recv1s.at[k], (to, grp)))
+    for copy in first:
+        copy.start()
+    slab[me] = cells_ref[col]
+    stat[me] = stats_ref[0]
+
+    second = []
+    other = lax.rem(grp + 1, groups)
+    for k in range(blocks):
+        if k:
+            first[2 * k - 2].wait_recv()
+            first[2 * k - 1].wait_recv()
+        came = lax.rem(col - k + blocks, blocks)
+        slot = came * groups + grp
+        source = cells_ref.at[col] if k == 0 else slab.at[slot]
+        source_s = stats_ref.at[0] if k == 0 else stat.at[slot]
+        pair = (remote(source, slab.at[slot], send2.at[k], recv2.at[k], (col, other)),
+                remote(source_s, stat.at[slot], send2s.at[k], recv2s.at[k], (col, other)))
+        for copy in pair:
+            copy.start()
+        second.extend(pair)
+    for copy in second:
+        copy.wait_recv()
+
+    bw = bw_ref[:, pl.ds(pl.multiple_of(col * span, span), span)].astype(jnp.float32)
+    near = docs // TILE
+    for o in range(owners // groups):
+        value = slab[grp * (owners // groups) + o].astype(jnp.float32) * bw
+        value = value.astype(jnp.bfloat16).astype(jnp.float32)
+        for t in range(near):
+            weighted[o * near + t] = value[t * TILE:(t + 1) * TILE]
+
+    third = []
+    for k in list(range(1, blocks)) + [0]:
+        block = lax.rem(col + k, blocks)
+        tiles = [weighted[cand_ref[0, block, c]] for c in range(picks)]
+        lines = jnp.concatenate(tiles, axis=0).astype(jnp.bfloat16)
+        columns = jnp.concatenate([slab[block * groups + o] for o in range(groups)], axis=0)
+        part[k] = lax.dot_general(columns, lines, NT, preferred_element_type=jnp.float32)
+        if k:
+            copy = remote(part.at[k], inbox.at[k], send3.at[k], recv3.at[k], (block, grp))
+            copy.start()
+            third.append(copy)
+
+    eight = lax.broadcasted_iota(jnp.int32, (TILE, LANES), 0)
+    lanes = lax.broadcasted_iota(jnp.int32, (TILE, LANES), 1)
+    pop_rows = jnp.zeros((TILE, LANES), jnp.float32)
+    size_rows = jnp.zeros((TILE, LANES), jnp.float32)
+    for c in range(picks):
+        tile = cand_ref[0, col, c]
+        line = stat[grp * (owners // groups) + lax.div(tile, near)]
+        spot = lanes - lax.rem(tile, near) * TILE - eight
+        pop = jnp.sum(jnp.where(spot == 0, line, 0.0), axis=1, keepdims=True)
+        size = jnp.sum(jnp.where(spot == docs, line, 0.0), axis=1, keepdims=True)
+        here = lanes == eight + c * TILE
+        pop_rows = jnp.where(here, pop, pop_rows)
+        size_rows = jnp.where(here, size, size_rows)
+    pop_rows = jnp.sum(pop_rows, axis=0, keepdims=True)
+    size_rows = jnp.sum(size_rows, axis=0, keepdims=True)
+    sub = lax.broadcasted_iota(jnp.int32, (docs, LANES), 0)
+    lane = lax.broadcasted_iota(jnp.int32, (docs, LANES), 1)
+    mine = [stat[col * groups + o] for o in range(groups)]
+    pop_cols = jnp.concatenate(
+        [jnp.sum(jnp.where(lane == sub, line, 0.0), axis=1, keepdims=True) for line in mine], axis=0)
+    size_cols = jnp.concatenate(
+        [jnp.sum(jnp.where(lane == sub + docs, line, 0.0), axis=1, keepdims=True) for line in mine], axis=0)
+
+    shared = part[0]
+    for k, copy in enumerate(third):
+        copy.wait_recv()
+        shared = shared + inbox[k + 1]
+    ratio = shared / (pop_rows + pop_cols - shared)
+    out_ref[...] = ratio * (size_rows + size_cols) / ((1.0 + ratio) * jnp.minimum(size_rows, size_cols))
+    for copy in first + second + third:
+        copy.wait_send()
+
+
+def fast_body(blocks, groups, positions, element_weights, set_sizes, bit_weights, candidates):
+    docs = positions.shape[0]
+    weights = bit_weights.reshape(1, -1)
+    cells, stats = make_filter(positions, element_weights, set_sizes, weights, blocks)
+    span = cells.shape[2]
+    width, rows = docs * groups, candidates.shape[2] * TILE
+    vmem = pl.BlockSpec(memory_space=pltpu.VMEM)
+    sems = lambda: pltpu.SemaphoreType.DMA((blocks,))
+    scores = pl.pallas_call(
+        functools.partial(score_kernel, blocks, groups),
+        out_shape=jax.ShapeDtypeStruct((width, rows), jnp.float32),
+        in_specs=[pl.BlockSpec(memory_space=pltpu.SMEM), vmem, vmem, vmem],
+        out_specs=vmem,
+        scratch_shapes=[
+            pltpu.VMEM((blocks * groups, docs, span), jnp.bfloat16),
+            pltpu.VMEM((blocks * groups, 1, LANES), jnp.float32),
+            pltpu.VMEM((docs * blocks // TILE, TILE, span), jnp.float32),
+            pltpu.VMEM((blocks, width, rows), jnp.float32),
+            pltpu.VMEM((blocks, width, rows), jnp.float32),
+        ] + [sems() for _ in range(10)],
+        compiler_params=pltpu.CompilerParams(collective_id=0, has_side_effects=True),
+    )(candidates, cells, stats.reshape(1, 1, LANES), weights)
+    return scores.T.reshape(1, 1, rows, width)
+
+
 def solution(mesh):
+    blocks, groups = mesh.shape["bits"], mesh.shape["docs"]
+    fits = groups == 2 and FILTER_BITS % (blocks * LANES) == 0
+    chosen = functools.partial(fast_body, blocks, groups) if fits else body
     return jax.shard_map(
-        body,
+        chosen,
         mesh=mesh,
         in_specs=(
             P(("bits", "docs"), None),

time: 159 us -> 50.2 us (0.32)
  the two profiles are of different devices: /device:TPU:0 before, /device:TPU:13 now
where the time goes in v1:
time: 50.2 us; the launch traced here: 49.9 us
  Pallas kernels  47.2 us (94%)
  local copies, waits for them, and re-layouts  2.69 us (5%)
    pallas_call x1, Pallas kernels, fast_body(): pl.pallas_call(functools.partial(score_kernel, blocks, groups), out_shape...  30.7 us
    pallas_call x1, Pallas kernels, make_filter(): pl.pallas_call(filter_kernel, out_shape=(jax.ShapeDtypeStruct((pieces, do...  16.5 us
    unnamed x1, local copies, waits for them, and re-layouts  1.38 us
    reshape x1, local copies, waits for them, and re-layouts, fast_body(): weights = bit_weights.reshape(1, -1)  1.31 us

profile of v1, /device:TPU:13, one launch (start us, length us, event | category | flops | bytes accessed | tf_op | source)
XLA Modules:
  0.0 49.9 jit_solution(2369705164282280581)
XLA Ops:
  0.0 1.3 %reshape.9.bw_ref = bf16[1,4096]{1,0:T(2,128)(2,1)} reshape(bf16[4096]{0:T(1024)(128)(2,1)} %param.8) | data formatting | bytes 16384 | tf_op jit(solution)/shard_map/reshape | solution.py:330
  1.3 16.5 %shard_map.55 = (bf16[16,32,256]{2,1,0:T(8,128)(2,1)}, f32[1,128]{1,0:T(1,128)}) custom-call(s32[32]{0:T(128)} %sizes_ref.1, s32[32,4096]{1,0:T(8,128)} %pos_ref.1, f32[32,1024]{1,0:T(8,128)} %elem_ref.1, bf16[1,4096]{1,0:T(2,128)(2,1)} %reshape.9.bw_ref), custom_call_target="tpu_custom_call" | custom-call | tf_op jit(solution)/shard_map/pallas_call | solution.py:209
  17.8 30.7 %shard_map.56 = f32[64,128]{1,0:T(8,128)} custom-call(s32[1,16,16]{2,1,0:T(8,128)} %cand_ref.1, bf16[16,32,256]{2,1,0:T(8,128)(2,1)} %get-tuple-element.7.cells_ref, f32[1,1,128]{2,1,0:T(1,128)} %bitcast.5, bf16[1,4096]{1,0:T(2,128)(2,1)} %reshape.9.bw_ref), custom_call_target="tpu_custom_call" | custom-call | tf_op jit(solution)/shard_map/pallas_call | solution.py:336
  48.6 1.4 %copy.7 = f32[1,1,128,64]{2,3,1,0:T(8,128)} copy(f32[1,1,128,64]{2,3,1,0:T(8,128)} %bitcast.4) | data formatting | bytes 65536
